TPU v7x, 32 devices: a whole 2x2x4 slice. The times are simulated.
32 devices in a mesh: row: 8 (over z, core), col: 4 (over y, x).
Axes of the slice: x: 2, y: 2, z: 4, core: 2. Of those that a mesh axis runs over, the one named last changes fastest.
Arguments:
- x_fwd: bfloat16 [512, 6144], P('row', 'col'), may hold values from -6 to 6
- x_bwd: bfloat16 [512, 6144], P('row', 'col'), may hold values from -6 to 6
- grad_out: bfloat16 [512, 6144], P('row', 'col'), may hold values from -1.5 to 1.5
- gain: float32 [6144], P('col'), may hold values from 0.1 to 1.9
- w_up: bfloat16 [6144, 12288], P('col', 'row'), may hold values from -0.078125 to 0.078125
- w_down: bfloat16 [12288, 6144], P('row', 'col'), may hold values from -0.0546875 to 0.0546875
Outputs:
- y_fwd: bfloat16 [512, 6144], P('row', 'col')
- dx_bwd: bfloat16 [512, 6144], P('row', 'col')
- step_up: float32 [6144, 12288], P('col', 'row')
- step_down: float32 [12288, 6144], P('row', 'col')
- step_gain: float32 [6144], P('col')
- grad_rms: float32 [], replicated
All inputs are finite; a program needn't handle non-finite values.
Results may differ from a plain program's by a relative error of at most 0.0017.
The roundings to bfloat16 on the way count: a program that leaves them out, or rounds other values in their place, can miss the bound.
Values may be sent and summed in bfloat16 or wider, within the bound.
A program may use at most 128 MiB of HBM per device.

v0:
```python
import math
import jax
import jax.numpy as jnp
from jax import lax
from jax.sharding import PartitionSpec as P

D = 6144
FF = 12288
eps = 1e-06
clip_share = 0.25


def erf_gelu(value):
    return 0.5 * value * (1.0 + lax.erf(value * 0.7071067811865476))


def gelu_slope(value):
    return (
        0.5 * (1.0 + lax.erf(value * 0.7071067811865476))
        + value * jnp.exp(-0.5 * value * value) * 0.3989422804014327
    )


def contract(left, right, left_dim, right_dim):
    return lax.dot_general(
        left, right, (((left_dim,), (right_dim,)), ((), ())), preferred_element_type=jnp.float32
    )


def row_sums(tokens):
    values = tokens.astype(jnp.float32)
    return (jnp.sum(values, -1), jnp.sum(values * values, -1))


def normalize(tokens, first, second):
    values = tokens.astype(jnp.float32)
    centre = first / D
    spread = second / D - centre * centre
    inv_scale = lax.rsqrt(spread + eps)
    return ((values - centre[:, None]) * inv_scale[:, None], inv_scale)


def up_both(normed_a, normed_b, w_up):
    full_a, full_b = (
        lax.all_gather(normed_a, "row", axis=0, tiled=True),
        lax.all_gather(normed_b, "row", axis=0, tiled=True),
    )
    width = w_up.shape[1]
    summed = lax.psum_scatter(
        jnp.concatenate(
            [
                jnp.dot(full_a, w_up, preferred_element_type=jnp.float32),
                jnp.dot(full_b, w_up, preferred_element_type=jnp.float32),
            ],
            1,
        ),
        "col",
        scatter_dimension=0,
        tiled=True,
    )
    return (summed[:, :width], summed[:, width:], full_b)


def on_device(x_fwd, x_bwd, grad_out, gain, w_up, w_down):
    first_a, second_a = row_sums(x_fwd)
    first_b, second_b = row_sums(x_bwd)
    first_a, second_a, first_b, second_b = lax.psum((first_a, second_a, first_b, second_b), "col")
    centred_a, _ = normalize(x_fwd, first_a, second_a)
    centred_b, inv_scale = normalize(x_bwd, first_b, second_b)
    normed_a = (centred_a * gain).astype(jnp.bfloat16)
    normed_b = (centred_b * gain).astype(jnp.bfloat16)
    pre_a, pre_b, normed_full = up_both(normed_a, normed_b, w_up)
    hidden_a = erf_gelu(pre_a).astype(jnp.bfloat16)
    output_part = jnp.dot(
        lax.all_gather(hidden_a, "col", axis=0, tiled=True),
        w_down,
        preferred_element_type=jnp.float32,
    )
    output_sum = lax.psum_scatter(output_part, "row", scatter_dimension=0, tiled=True)
    y_fwd = (x_fwd.astype(jnp.float32) + output_sum).astype(jnp.bfloat16)
    hidden_b = erf_gelu(pre_b).astype(jnp.bfloat16)
    grad_full = lax.all_gather(grad_out, "row", axis=0, tiled=True)
    grad_hidden = lax.psum_scatter(
        contract(grad_full, w_down, 1, 1), "col", scatter_dimension=0, tiled=True
    )
    grad_pre = (grad_hidden * gelu_slope(pre_b)).astype(jnp.bfloat16)
    hidden_piece = lax.all_gather(hidden_b, "col", axis=0, tiled=True)
    pre_piece = lax.all_gather(grad_pre, "col", axis=0, tiled=True)
    down_total = contract(hidden_piece, grad_full, 0, 0)
    up_total = contract(normed_full, pre_piece, 0, 0)
    input_total = contract(pre_piece, w_up, 1, 1)
    grad_normed = lax.psum_scatter(input_total, "row", scatter_dimension=0, tiled=True)
    scaled = grad_normed * gain
    first_back = jnp.sum(scaled, -1)
    second_back = jnp.sum(scaled * centred_b, -1)
    first_back, second_back = lax.psum((first_back, second_back), "col")
    dx_bwd = (
        grad_out.astype(jnp.float32)
        + inv_scale[:, None]
        * (scaled - first_back[:, None] / D - centred_b * (second_back[:, None] / D))
    ).astype(jnp.bfloat16)
    gain_part = jnp.sum(grad_normed * centred_b, 0)
    weight_squares = jnp.sum(up_total * up_total) + jnp.sum(down_total * down_total)
    g_gain = lax.psum(gain_part, "row")
    first_row = (lax.axis_index("row") == 0).astype(jnp.float32)
    total = lax.psum(weight_squares + first_row * jnp.sum(g_gain * g_gain), ("row", "col"))
    param_count = 2 * D * FF + D
    norm_value = jnp.sqrt(total)
    grad_rms = norm_value / math.sqrt(param_count)
    factor = jnp.minimum(1.0, clip_share * math.sqrt(param_count) / norm_value)
    return (y_fwd, dx_bwd, up_total * factor, down_total * factor, g_gain * factor, grad_rms)


def solution(mesh):
    placed = (
        P("row", "col"),
        P("row", "col"),
        P("row", "col"),
        P("col"),
        P("col", "row"),
        P("row", "col"),
    )
    return jax.shard_map(
        on_device,
        mesh=mesh,
        in_specs=placed,
        out_specs=(
            P("row", "col"),
            P("row", "col"),
            P("col", "row"),
            P("row", "col"),
            P("col"),
            P(),
        ),
        check_vma=False,
    )
```

profile of v0, /device:TPU:0, one launch (start us, length us, event | category | flops | bytes accessed | tf_op | source)
XLA Modules:
  0.0 446.6 jit_solution(12459251885347289089)
XLA Ops:
  7.2 0.0 all-gather.13.cloned.1.call-start
  7.2 0.7 all-gather.13.cloned.1.call-update
  7.9 0.0 all-gather.7.cloned.1.call-start
  7.9 1.1 convert_reduce_fusion
  9.0 1.1 convert_reduce_fusion.1
  10.1 11.4 %all-reduce.1 = (f32[64]{0:T(128)S(1)}, f32[64]{0:T(128)S(1)}, f32[64]{0:T(128)S(1)}, f32[64]{0:T(128)S(1)}) all-reduce(f32[64]{0:T(128)S(1)} %get-tuple-element.12, f32[64]{0:T(128)S(1)} %get-tuple-element.11, f32[64]{0:T(128)S(1)} %get-tuple-element.10, f32[64]{0:T(128)S(1)} %get-tuple-element.9), channel_id=1, replica_groups=mesh['row'=8,'col'=4] {'col'}, use_global_device_ids=true, to_apply=%region_7.0 | all-reduce | flops 256 | bytes 2048 | tf_op jit(solution)/shard_map/psum | solution.py:67
  21.5 2.0 fusion.21
  23.6 0.0 all-gather.9.cloned.1.call-start
  23.6 0.7 all-gather.9.cloned.1.call-update
  24.3 0.0 reduce-scatter.9.cloned.1.call-start
  24.4 13.3 %all-gather.13.cloned.1.call-done = bf16[512,1536]{1,0:T(8,128)(2,1)} async-done(((bf16[64,1536]{1,0:T(8,128)(2,1)}), bf16[512,1536]{1,0:T(8,128)(2,1)}) %all-gather.13.cloned.1.call-update) | async-done | bytes 1572880 | tf_op jit(solution)/shard_map/all_gather | solution.py:82
  37.6 7.1 %fusion.27 = f32[512,1536]{1,0:T(8,128)} fusion(bf16[512,1536]{1,0:T(8,128)(2,1)} %all-gather.13.cloned.1.call-done, bf16[1536,1536]{1,0:T(8,128)(2,1)} %param.11), kind=kOutput, calls=%fused_computation.52 | convolution fusion | flops 2415919104 | bytes 9437184 | tf_op jit(solution)/shard_map/dot_general | solution.py:25
  44.8 0.0 reduce-scatter.5.cloned.1.call-start
  44.8 19.4 %all-gather.7.cloned.1.call-done = bf16[512,1536]{1,0:T(8,128)(2,1)} async-done(((bf16[64,1536]{1,0:T(8,128)(2,1)}), bf16[512,1536]{1,0:T(8,128)(2,1)}) %all-gather.7.cloned.1.call-update) | async-done | bytes 1572880 | tf_op jit(solution)/shard_map/all_gather | solution.py:45
  64.3 4.9 %fusion.24 = f32[512,1536]{1,0:T(8,128)S(1)} fusion(bf16[512,1536]{1,0:T(8,128)(2,1)} %all-gather.7.cloned.1.call-done, bf16[1536,1536]{1,0:T(8,128)(2,1)} %param.10), kind=kOutput, calls=%fused_computation.49 | convolution fusion | flops 2415919104 | bytes 9437184 | tf_op jit(solution)/shard_map/dot_general | solution.py:52
  69.2 21.7 %all-gather.9.cloned.1.call-done = bf16[512,1536]{1,0:T(8,128)(2,1)} async-done(((bf16[64,1536]{1,0:T(8,128)(2,1)}), bf16[512,1536]{1,0:T(8,128)(2,1)}) %all-gather.9.cloned.1.call-update) | async-done | bytes 1572880 | tf_op jit(solution)/shard_map/all_gather | solution.py:46
  90.9 4.9 %fusion.25 = f32[512,1536]{1,0:T(8,128)S(1)} fusion(bf16[512,1536]{1,0:T(8,128)(2,1)} %all-gather.9.cloned.1.call-done, bf16[1536,1536]{1,0:T(8,128)(2,1)} %param.10), kind=kOutput, calls=%fused_computation.50 | convolution fusion | flops 2415919104 | bytes 9437184 | tf_op jit(solution)/shard_map/dot_general | solution.py:53
  95.9 3.3 pad_maximum_fusion
  99.1 0.0 all-gather.15.cloned.1.call-start
  99.2 38.2 %reduce-scatter.9.cloned.1.call-done = f32[128,1536]{1,0:T(8,128)} async-done(((f32[512,1536]{1,0:T(8,128)}), f32[128,1536]{1,0:T(8,128)}) %reduce-scatter.9.cloned.1.call-update) | async-done | bytes 786448 | tf_op jit(solution)/shard_map/reduce_scatter | solution.py:83
  137.4 73.5 %reduce-scatter.5.cloned.1.call-done = f32[128,3072]{1,0:T(8,128)} async-done(((f32[512,3072]{1,0:T(8,128)}), f32[128,3072]{1,0:T(8,128)}) %reduce-scatter.5.cloned.1.call-update) | async-done | bytes 1572880 | tf_op jit(solution)/shard_map/reduce_scatter | solution.py:49
  210.9 3.0 multiply_convert_fusion
  213.9 0.0 all-gather.11.cloned.1.call-start
  214.0 0.7 all-gather.11.cloned.1.call-update
  214.7 0.0 all-gather.17.cloned.1.call-start
  214.7 0.7 all-gather.17.cloned.1.call-update
  215.4 0.0 reduce-scatter.11.cloned.1.call-start
  215.5 29.5 %all-gather.15.cloned.1.call-done = bf16[512,1536]{1,0:T(8,128)(2,1)} async-done(((bf16[128,1536]{1,0:T(8,128)(2,1)}), bf16[512,1536]{1,0:T(8,128)(2,1)}) %all-gather.15.cloned.1.call-update) | async-done | bytes 1572880 | tf_op jit(solution)/shard_map/all_gather | solution.py:88
  244.9 7.1 %fusion.28 = f32[512,1536]{1,0:T(8,128)} fusion(bf16[512,1536]{1,0:T(8,128)(2,1)} %all-gather.15.cloned.1.call-done, bf16[1536,1536]{1,0:T(8,128)(2,1)} %param.10), kind=kOutput, calls=%fused_computation.53 | convolution fusion | flops 2415919104 | bytes 9437184 | tf_op jit(solution)/shard_map/dot_general | solution.py:25
  252.1 0.2 reduce-scatter.7.cloned.1.call-start
  252.3 25.3 %all-gather.11.cloned.1.call-done = bf16[512,1536]{1,0:T(8,128)(2,1)} async-done(((bf16[128,1536]{1,0:T(8,128)(2,1)}), bf16[512,1536]{1,0:T(8,128)(2,1)}) %all-gather.11.cloned.1.call-update) | async-done | bytes 1572880 | tf_op jit(solution)/shard_map/all_gather | solution.py:75
  277.6 7.1 %fusion.26 = f32[512,1536]{1,0:T(8,128)} fusion(bf16[512,1536]{1,0:T(8,128)(2,1)} %all-gather.11.cloned.1.call-done, bf16[1536,1536]{1,0:T(8,128)(2,1)} %param.11), kind=kOutput, calls=%fused_computation.51 | convolution fusion | flops 2415919104 | bytes 9437184 | tf_op jit(solution)/shard_map/dot_general | solution.py:74
  284.8 1.4 copy-done.5
  286.2 0.5 copy-done.6
  286.7 6.0 %multiply_reduce_fusion.1 = (f32[]{:T(128)}, f32[1536,1536]{1,0:T(8,128)}) fusion(bf16[512,1536]{1,0:T(8,128)(2,1)S(1)} %copy-done.5, bf16[512,1536]{1,0:T(8,128)(2,1)S(1)} %copy-done.6), kind=kOutput, calls=%fused_computation.1 | convolution fusion | flops 2420637696 | bytes 12582916 | tf_op jit(solution)/shard_map/dot_general | solution.py:25
  292.7 18.2 %all-gather.17.cloned.1.call-done = bf16[512,1536]{1,0:T(8,128)(2,1)} async-done(((bf16[128,1536]{1,0:T(8,128)(2,1)}), bf16[512,1536]{1,0:T(8,128)(2,1)}) %all-gather.17.cloned.1.call-update) | async-done | bytes 1572880 | tf_op jit(solution)/shard_map/all_gather | solution.py:87
  310.9 8.9 %multiply_reduce_fusion = (f32[]{:T(128)}, f32[1536,1536]{1,0:T(8,128)}) fusion(bf16[512,1536]{1,0:T(8,128)(2,1)} %all-gather.17.cloned.1.call-done, bf16[512,1536]{1,0:T(8,128)(2,1)} %all-gather.13.cloned.1.call-done), kind=kOutput, calls=%fused_computation | convolution fusion | flops 2420637696 | bytes 12582916 | tf_op jit(solution)/shard_map/dot_general | solution.py:25
  321.1 32.5 %reduce-scatter.11.cloned.1.call-done = f32[64,1536]{1,0:T(8,128)} async-done(((f32[512,1536]{1,0:T(8,128)}), f32[64,1536]{1,0:T(8,128)}) %reduce-scatter.11.cloned.1.call-update) | async-done | bytes 393232 | tf_op jit(solution)/shard_map/reduce_scatter | solution.py:92
  353.6 1.4 fusion.17
  355.0 16.1 %psum.62 = f32[1536]{0:T(1024)S(1)} all-reduce(f32[1536]{0:T(1024)S(1)} %get-tuple-element.6), channel_id=1, replica_groups=mesh['row'=8,'col'=4] {'row'}, use_global_device_ids=true, to_apply=%region_19.0 | all-reduce | flops 1536 | bytes 12288 | tf_op jit(solution)/shard_map/psum | solution.py:104
  371.1 0.6 multiply_reduce_fusion.3
  372.3 38.8 %psum.63 = f32[]{:T(128)} all-reduce(f32[]{:T(128)S(6)} %add.60), channel_id=1, replica_groups=mesh['row'=8,'col'=4] {'row','col'}, use_global_device_ids=true, to_apply=%region_21.0 | all-reduce | flops 1 | bytes 8 | tf_op jit(solution)/shard_map/psum | solution.py:106
  411.9 9.9 %all-reduce = (f32[64]{0:T(128)S(1)}, f32[64]{0:T(128)S(1)}) all-reduce(f32[64]{0:T(128)S(1)} %get-tuple-element.7, f32[64]{0:T(128)S(1)} %get-tuple-element.8), channel_id=1, replica_groups=mesh['row'=8,'col'=4] {'col'}, use_global_device_ids=true, to_apply=%region_15.0 | all-reduce | flops 128 | bytes 1024 | tf_op jit(solution)/shard_map/psum | solution.py:96
  421.8 0.6 broadcast_multiply_fusion.2
  422.5 8.7 %broadcast_multiply_fusion = f32[1536,1536]{1,0:T(8,128)} fusion(f32[1536,1536]{1,0:T(8,128)} %get-tuple-element.31, f32[]{:T(128)S(6)} %min.3), kind=kLoop, calls=%fused_computation.3 | loop fusion | flops 2359296 | bytes 18874372 | tf_op jit(solution)/shard_map/mul | solution.py:111
  431.2 4.8 %broadcast_multiply_fusion.1 = f32[1536,1536]{1,0:T(8,128)} fusion(f32[1536,1536]{1,0:T(8,128)S(1)} %bitcast.15, f32[]{:T(128)S(6)} %min.3), kind=kLoop, calls=%fused_computation.4 | loop fusion | flops 2359296 | bytes 18874372 | tf_op jit(solution)/shard_map/mul | solution.py:111
  436.0 1.7 fusion.23
  437.7 0.9 fusion.16
  (29 shorter events, 0.2 us)
Async XLA Ops:
  7.2 30.5 %all-gather.13.cloned.1.call-start = ((), (), s32[]{:S(2)}) async-start(), calls=%async_computation.9 | async-start | bytes 1769472 | tf_op jit(solution)/shard_map/all_gather | solution.py:82
  7.9 56.4 %all-gather.7.cloned.1.call-start = ((), (), s32[]{:S(2)}) async-start(), calls=%async_computation.4 | async-start | bytes 1769472 | tf_op jit(solution)/shard_map/all_gather | solution.py:45
  23.6 67.3 %all-gather.9.cloned.1.call-start = ((), (), s32[]{:S(2)}) async-start(), calls=%async_computation.5 | async-start | bytes 1769472 | tf_op jit(solution)/shard_map/all_gather | solution.py:46
  24.3 113.1 %reduce-scatter.9.cloned.1.call-start = ((), (), s32[]{:S(2)}) async-start(), calls=%async_computation.10 | async-start | bytes 3932160 | tf_op jit(solution)/shard_map/reduce_scatter | solution.py:83
  44.8 166.1 %reduce-scatter.5.cloned.1.call-start = ((), (), s32[]{:S(2)}) async-start(), calls=%async_computation.6 | async-start | bytes 7864320 | tf_op jit(solution)/shard_map/reduce_scatter | solution.py:49
  99.1 145.8 %all-gather.15.cloned.1.call-start = ((), (), s32[]{:S(2)}) async-start(), calls=%async_computation.11 | async-start | bytes 1966080 | tf_op jit(solution)/shard_map/all_gather | solution.py:88
  213.9 63.7 %all-gather.11.cloned.1.call-start = ((), (), s32[]{:S(2)}) async-start(), calls=%async_computation.7 | async-start | bytes 1966080 | tf_op jit(solution)/shard_map/all_gather | solution.py:75
  214.7 96.2 %all-gather.17.cloned.1.call-start = ((), (), s32[]{:S(2)}) async-start(), calls=%async_computation.13 | async-start | bytes 1966080 | tf_op jit(solution)/shard_map/all_gather | solution.py:87
  215.4 138.2 %reduce-scatter.11.cloned.1.call-start = ((), (), s32[]{:S(2)}) async-start(), calls=%async_computation.12 | async-start | bytes 3538944 | tf_op jit(solution)/shard_map/reduce_scatter | solution.py:92
  252.1 183.9 %reduce-scatter.7.cloned.1.call-start = ((), (), s32[]{:S(2)}) async-start(), calls=%async_computation.8 | async-start | bytes 3538944 | tf_op jit(solution)/shard_map/reduce_scatter | solution.py:79
  284.8 1.4 copy-start.5
  284.8 1.9 copy-start.6
  292.7 60.9 %copy-start = (bf16[64,1536]{1,0:T(8,128)(2,1)S(1)}, bf16[64,1536]{1,0:T(8,128)(2,1)}, u32[]{:S(2)}) copy-start(bf16[64,1536]{1,0:T(8,128)(2,1)} %param.7) | copy-start | bytes 589828
  292.7 60.9 %copy-start.4 = (f32[1536]{0:T(1024)S(1)}, f32[1536]{0:T(1024)}, u32[]{:S(2)}) copy-start(f32[1536]{0:T(1024)} %param.9) | copy-start | bytes 18436
  353.6 77.5 %slice-start = ((s8[9437184]{0:T(1024)(128)(4,1)}), s8[1048576]{0:T(1024)(128)(4,1)S(1)}, s32[]{:S(2)}) async-start(s8[9437184]{0:T(1024)(128)(4,1)} %bitcast.14), calls=%async_computation.14 | async-start | bytes 2097152
  422.4 8.7 %slice-start.1 = ((s8[9437184]{0:T(1024)(128)(4,1)}), s8[4194304]{0:T(1024)(128)(4,1)S(1)}, s32[]{:S(2)}) async-start(s8[9437184]{0:T(1024)(128)(4,1)} %bitcast.14), calls=%async_computation.15 | async-start | bytes 8388608
  422.4 8.7 %slice-start.2 = ((s8[9437184]{0:T(1024)(128)(4,1)}), s8[4194304]{0:T(1024)(128)(4,1)S(1)}, s32[]{:S(2)}) async-start(s8[9437184]{0:T(1024)(128)(4,1)} %bitcast.14), calls=%async_computation.16 | async-start | bytes 8388608
  431.1 4.8 %copy-start.1 = (bf16[64,1536]{1,0:T(8,128)(2,1)S(1)}, bf16[64,1536]{1,0:T(8,128)(2,1)}, u32[]{:S(2)}) copy-start(bf16[64,1536]{1,0:T(8,128)(2,1)} %param.6) | copy-start | bytes 589828
  431.2 6.5 %copy-start.2 = (f32[64,1536]{1,0:T(8,128)S(1)}, f32[64,1536]{1,0:T(8,128)}, u32[]{:S(2)}) copy-start(f32[64,1536]{1,0:T(8,128)} %reduce-scatter.11.cloned.1.call-done) | copy-start | bytes 1179652
  431.2 6.5 %copy-start.3 = (bf16[64,1536]{1,0:T(8,128)(2,1)S(1)}, bf16[64,1536]{1,0:T(8,128)(2,1)}, u32[]{:S(2)}) copy-start(bf16[64,1536]{1,0:T(8,128)(2,1)} %param.8) | copy-start | bytes 589828
Sparse Core Ops, SparseCore 0:
  9.6 27.9 all-gather.12
  39.8 24.3 all-gather.6
  66.5 24.3 all-gather.8
  94.3 43.0 reduce-scatter.8
  140.8 70.0 reduce-scatter.4
  214.0 30.8 all-gather.14
  246.8 30.8 all-gather.10
  280.0 30.8 all-gather.16
  313.2 40.3 reduce-scatter.10
  355.8 40.2 reduce-scatter.6
where the time goes:
time: 447 us
  waiting for transfers between devices  274 us (61%)
  blocking collectives  76.2 us (17%)
  matrix products  46.1 us (10%)
  other arithmetic  29.2 us (7%)
  between operations  18.1 us (4%)
    reduce_scatter x1, waiting for transfers between devices, up_both(): lax.psum_scatter(jnp.concatenate([jnp.dot(full_a, w_up, preferred_element...  73.5 us
    psum x1, blocking collectives, on_device(): lax.psum(weight_squares + first_row * jnp.sum(g_gain * g_gain), ('row', '...  38.8 us
    reduce_scatter x1, waiting for transfers between devices, on_device(): lax.psum_scatter(contract(grad_full, w_down, 1, 1), 'col', scatter_dimens...  38.2 us
    reduce_scatter x1, waiting for transfers between devices, on_device(): lax.psum_scatter(input_total, 'row', scatter_dimension=0, tiled=True)  32.5 us
    all_gather x1, waiting for transfers between devices, on_device(): pre_piece = lax.all_gather(grad_pre, 'col', axis=0, tiled=True)  29.5 us
    dot_general x4, matrix products, contract(): lax.dot_general(left, right, (((left_dim,), (right_dim,)), ((), ())), pre...  29.2 us
    all_gather x1, waiting for transfers between devices, on_device(): lax.all_gather(hidden_a, 'col', axis=0, tiled=True)  25.3 us
    all_gather x1, waiting for transfers between devices, up_both(): lax.all_gather(normed_b, 'row', axis=0, tiled=True)  21.7 us
  transfers between devices with their start and end apart: 10, of which 9 were waited for; matrix products, arithmetic and copies ran while one was open for 16% of the time, Pallas kernels for 0%

commit v1 on v0

--- a/solution.py
+++ b/solution.py
@@ -85,7 +85,12 @@
     )
     grad_pre = (grad_hidden * gelu_slope(pre_b)).astype(jnp.bfloat16)
     hidden_piece = lax.all_gather(hidden_b, "col", axis=0, tiled=True)
-    pre_piece = lax.all_gather(grad_pre, "col", axis=0, tiled=True)
+    ring = [grad_pre]
+    for hop in range(3):
+        ring.append(lax.ppermute(ring[-1], "col", [(dev, (dev + 1) % 4) for dev in range(4)]))
+    pre_piece = jnp.roll(
+        jnp.concatenate(ring[::-1], axis=0), (lax.axis_index("col") + 1) * ring[0].shape[0], axis=0
+    )
     down_total = contract(hidden_piece, grad_full, 0, 0)
     up_total = contract(normed_full, pre_piece, 0, 0)
     input_total = contract(pre_piece, w_up, 1, 1)

time: 447 us -> 424 us (0.949)
  waiting for transfers between devices: 274 us -> 243 us
  starting transfers between devices: 0.58 us -> 5.42 us
    ppermute x0 -> x3, waiting for transfers between devices: none -> 37.2 us  [on_device(): lax.ppermute(ring[-1], 'col', [(dev, (dev + 1) % 4) for dev in range(4)])]
    all_gather x1 -> x0, waiting for transfers between devices: 29.5 us -> none  [on_device(): pre_piece = lax.all_gather(grad_pre, 'col', axis=0, tiled=True)]
    all_gather x1, waiting for transfers between devices: 25.3 us -> 0.02 us  [on_device(): lax.all_gather(hidden_a, 'col', axis=0, tiled=True)]
    all_gather x1, waiting for transfers between devices: 18.2 us -> 5.23 us  [on_device(): hidden_piece = lax.all_gather(hidden_b, 'col', axis=0, tiled=True)]
    ppermute x0 -> x3, starting transfers between devices: none -> 4.87 us  [on_device(): lax.ppermute(ring[-1], 'col', [(dev, (dev + 1) % 4) for dev in range(4)])]
  transfers between devices with their start and end apart: 10 -> 12, of which waited for: 9 -> 10; matrix products, arithmetic and copies ran while one was open for 16% -> 17% of each run, Pallas kernels for 0% -> 0%
where the time goes in v1:
time: 424 us; the launch traced here: 423 us
  waiting for transfers between devices  243 us (57%)
  blocking collectives  76.2 us (18%)
  matrix products  47.1 us (11%)
  other arithmetic  30.2 us (7%)
  between operations  17.8 us (4%)
  starting transfers between devices  5.42 us (1%)
    reduce_scatter x1, waiting for transfers between devices, up_both(): lax.psum_scatter(jnp.concatenate([jnp.dot(full_a, w_up, preferred_element...  73.5 us
    psum x1, blocking collectives, on_device(): lax.psum(weight_squares + first_row * jnp.sum(g_gain * g_gain), ('row', '...  38.5 us
    reduce_scatter x1, waiting for transfers between devices, on_device(): lax.psum_scatter(contract(grad_full, w_down, 1, 1), 'col', scatter_dimens...  38.2 us
    ppermute x3, waiting for transfers between devices, on_device(): lax.ppermute(ring[-1], 'col', [(dev, (dev + 1) % 4) for dev in range(4)])  37.2 us
    reduce_scatter x1, waiting for transfers between devices, on_device(): lax.psum_scatter(input_total, 'row', scatter_dimension=0, tiled=True)  32.5 us
    dot_general x4, matrix products, contract(): lax.dot_general(left, right, (((left_dim,), (right_dim,)), ((), ())), pre...  30.1 us
    all_gather x1, waiting for transfers between devices, up_both(): lax.all_gather(normed_b, 'row', axis=0, tiled=True)  21.7 us
    all_gather x1, waiting for transfers between devices, up_both(): lax.all_gather(normed_a, 'row', axis=0, tiled=True)  19.4 us
  transfers between devices with their start and end apart: 12, of which 10 were waited for; matrix products, arithmetic and copies ran while one was open for 17% of the time, Pallas kernels for 0%

profile of v1, /device:TPU:0, one launch (start us, length us, event | category | flops | bytes accessed | tf_op | source)
XLA Modules:
  0.0 423.0 jit_solution(10006739307052160839)
XLA Ops:
  7.2 0.7 all-gather.12.cloned.1.call-update
  7.9 0.0 all-gather.6.cloned.1.call-start
  7.9 1.1 convert_reduce_fusion
  9.0 1.1 convert_reduce_fusion.1
  10.1 11.4 %all-reduce.1 = (f32[64]{0:T(128)S(1)}, f32[64]{0:T(128)S(1)}, f32[64]{0:T(128)S(1)}, f32[64]{0:T(128)S(1)}) all-reduce(f32[64]{0:T(128)S(1)} %get-tuple-element.12, f32[64]{0:T(128)S(1)} %get-tuple-element.11, f32[64]{0:T(128)S(1)} %get-tuple-element.10, f32[64]{0:T(128)S(1)} %get-tuple-element.9), channel_id=1, replica_groups=mesh['row'=8,'col'=4] {'col'}, use_global_device_ids=true, to_apply=%region_7.0 | all-reduce | flops 256 | bytes 2048 | tf_op jit(solution)/shard_map/psum | solution.py:67
  21.5 2.0 fusion.25
  23.6 0.0 all-gather.8.cloned.1.call-start
  23.6 0.7 all-gather.8.cloned.1.call-update
  24.3 0.0 reduce-scatter.9.cloned.1.call-start
  24.4 13.3 %all-gather.12.cloned.1.call-done = bf16[512,1536]{1,0:T(8,128)(2,1)} async-done(((bf16[64,1536]{1,0:T(8,128)(2,1)}), bf16[512,1536]{1,0:T(8,128)(2,1)}) %all-gather.12.cloned.1.call-update) | async-done | bytes 1572880 | tf_op jit(solution)/shard_map/all_gather | solution.py:82
  37.6 7.1 %fusion.33 = f32[512,1536]{1,0:T(8,128)} fusion(bf16[512,1536]{1,0:T(8,128)(2,1)} %all-gather.12.cloned.1.call-done, bf16[1536,1536]{1,0:T(8,128)(2,1)} %param.11), kind=kOutput, calls=%fused_computation.66 | convolution fusion | flops 2415919104 | bytes 9437184 | tf_op jit(solution)/shard_map/dot_general | solution.py:25
  44.8 0.0 reduce-scatter.5.cloned.1.call-start
  44.8 19.4 %all-gather.6.cloned.1.call-done = bf16[512,1536]{1,0:T(8,128)(2,1)} async-done(((bf16[64,1536]{1,0:T(8,128)(2,1)}), bf16[512,1536]{1,0:T(8,128)(2,1)}) %all-gather.6.cloned.1.call-update) | async-done | bytes 1572880 | tf_op jit(solution)/shard_map/all_gather | solution.py:45
  64.3 4.9 %fusion.30 = f32[512,1536]{1,0:T(8,128)S(1)} fusion(bf16[512,1536]{1,0:T(8,128)(2,1)} %all-gather.6.cloned.1.call-done, bf16[1536,1536]{1,0:T(8,128)(2,1)} %param.10), kind=kOutput, calls=%fused_computation.63 | convolution fusion | flops 2415919104 | bytes 9437184 | tf_op jit(solution)/shard_map/dot_general | solution.py:52
  69.2 21.7 %all-gather.8.cloned.1.call-done = bf16[512,1536]{1,0:T(8,128)(2,1)} async-done(((bf16[64,1536]{1,0:T(8,128)(2,1)}), bf16[512,1536]{1,0:T(8,128)(2,1)}) %all-gather.8.cloned.1.call-update) | async-done | bytes 1572880 | tf_op jit(solution)/shard_map/all_gather | solution.py:46
  90.9 4.9 %fusion.31 = f32[512,1536]{1,0:T(8,128)S(1)} fusion(bf16[512,1536]{1,0:T(8,128)(2,1)} %all-gather.8.cloned.1.call-done, bf16[1536,1536]{1,0:T(8,128)(2,1)} %param.10), kind=kOutput, calls=%fused_computation.64 | convolution fusion | flops 2415919104 | bytes 9437184 | tf_op jit(solution)/shard_map/dot_general | solution.py:53
  95.9 3.3 pad_maximum_fusion
  99.1 0.0 all-gather.10.cloned.1.call-start
  99.2 38.2 %reduce-scatter.9.cloned.1.call-done = f32[128,1536]{1,0:T(8,128)} async-done(((f32[512,1536]{1,0:T(8,128)}), f32[128,1536]{1,0:T(8,128)}) %reduce-scatter.9.cloned.1.call-update) | async-done | bytes 786448 | tf_op jit(solution)/shard_map/reduce_scatter | solution.py:83
  137.4 73.5 %reduce-scatter.5.cloned.1.call-done = f32[128,3072]{1,0:T(8,128)} async-done(((f32[512,3072]{1,0:T(8,128)}), f32[128,3072]{1,0:T(8,128)}) %reduce-scatter.5.cloned.1.call-update) | async-done | bytes 1572880 | tf_op jit(solution)/shard_map/reduce_scatter | solution.py:49
  210.9 3.0 multiply_convert_fusion
  213.9 0.0 all-gather.14.cloned.1.call-start
  213.9 1.5 collective-permute-start
  215.5 11.5 %collective-permute-done = bf16[128,1536]{1,0:T(8,128)(2,1)S(1)} collective-permute-done((bf16[128,1536]{1,0:T(8,128)(2,1)S(1)}, bf16[128,1536]{1,0:T(8,128)(2,1)S(1)}, u32[]{:S(2)}, u32[]{:S(2)}) %collective-permute-start) | collective-permute-done | bytes 393248 | tf_op jit(solution)/shard_map/ppermute | solution.py:90
  227.0 2.5 collective-permute-start.1
  229.5 8.8 %collective-permute-done.1 = bf16[128,1536]{1,0:T(8,128)(2,1)S(1)} collective-permute-done((bf16[128,1536]{1,0:T(8,128)(2,1)S(1)}, bf16[128,1536]{1,0:T(8,128)(2,1)S(1)}, u32[]{:S(2)}, u32[]{:S(2)}) %collective-permute-start.1) | collective-permute-done | bytes 393248 | tf_op jit(solution)/shard_map/ppermute | solution.py:90
  238.2 0.9 collective-permute-start.2
  239.1 0.0 reduce-scatter.11.cloned.1.call-start
  239.2 16.9 %collective-permute-done.2 = bf16[128,1536]{1,0:T(8,128)(2,1)S(1)} collective-permute-done((bf16[128,1536]{1,0:T(8,128)(2,1)S(1)}, bf16[128,1536]{1,0:T(8,128)(2,1)S(1)}, u32[]{:S(2)}, u32[]{:S(2)}) %collective-permute-start.2) | collective-permute-done | bytes 393248 | tf_op jit(solution)/shard_map/ppermute | solution.py:90
  256.4 1.7 copy-done.4
  258.0 6.7 %fusion.2 = f32[512,1536]{1,0:T(8,128)} fusion(bf16[1536,1536]{1,0:T(8,128)(2,1)} %param.10, bf16[1024,1536]{1,0:T(8,128)(2,1)S(1)} %constant_dynamic-update-slice_fusion, s32[]{:T(128)S(6)} %select_n.14), kind=kOutput, calls=%fused_computation.7 | convolution fusion | flops 2415919104 | bytes 9437188 | tf_op jit(solution)/shard_map/dot_general | solution.py:25
  264.7 0.2 reduce-scatter.7.cloned.1.call-start
  265.0 7.1 %fusion.32 = f32[512,1536]{1,0:T(8,128)} fusion(bf16[512,1536]{1,0:T(8,128)(2,1)} %all-gather.10.cloned.1.call-done, bf16[1536,1536]{1,0:T(8,128)(2,1)} %param.11), kind=kOutput, calls=%fused_computation.65 | convolution fusion | flops 2415919104 | bytes 9437184 | tf_op jit(solution)/shard_map/dot_general | solution.py:74
  272.1 1.9 copy-done.5
  274.0 7.5 %multiply_reduce_fusion.1 = (f32[]{:T(128)}, f32[1536,1536]{1,0:T(8,128)}) fusion(bf16[512,1536]{1,0:T(8,128)(2,1)} %all-gather.8.cloned.1.call-done, bf16[1024,1536]{1,0:T(8,128)(2,1)S(1)} %copy-done.5, s32[]{:T(128)S(6)} %select_n.14), kind=kOutput, calls=%fused_computation.1 | convolution fusion | flops 2420637696 | bytes 12582920 | tf_op jit(solution)/shard_map/dot_general | solution.py:25
  281.4 5.2 %all-gather.14.cloned.1.call-done = bf16[512,1536]{1,0:T(8,128)(2,1)} async-done(((bf16[128,1536]{1,0:T(8,128)(2,1)}), bf16[512,1536]{1,0:T(8,128)(2,1)}) %all-gather.14.cloned.1.call-update) | async-done | bytes 1572880 | tf_op jit(solution)/shard_map/all_gather | solution.py:87
  286.7 8.9 %multiply_reduce_fusion = (f32[]{:T(128)}, f32[1536,1536]{1,0:T(8,128)}) fusion(bf16[512,1536]{1,0:T(8,128)(2,1)} %all-gather.14.cloned.1.call-done, bf16[512,1536]{1,0:T(8,128)(2,1)} %all-gather.12.cloned.1.call-done), kind=kOutput, calls=%fused_computation | convolution fusion | flops 2420637696 | bytes 12582916 | tf_op jit(solution)/shard_map/dot_general | solution.py:25
  296.8 32.5 %reduce-scatter.11.cloned.1.call-done = f32[64,1536]{1,0:T(8,128)} async-done(((f32[512,1536]{1,0:T(8,128)}), f32[64,1536]{1,0:T(8,128)}) %reduce-scatter.11.cloned.1.call-update) | async-done | bytes 393232 | tf_op jit(solution)/shard_map/reduce_scatter | solution.py:97
  329.4 1.3 fusion.21
  330.6 16.2 %psum.62 = f32[1536]{0:T(1024)S(1)} all-reduce(f32[1536]{0:T(1024)S(1)} %get-tuple-element.6), channel_id=1, replica_groups=mesh['row'=8,'col'=4] {'row'}, use_global_device_ids=true, to_apply=%region_19.20 | all-reduce | flops 1536 | bytes 12288 | tf_op jit(solution)/shard_map/psum | solution.py:109
  346.8 0.6 multiply_reduce_fusion.3
  348.1 38.5 %psum.63 = f32[]{:T(128)} all-reduce(f32[]{:T(128)S(6)} %add.76), channel_id=1, replica_groups=mesh['row'=8,'col'=4] {'row','col'}, use_global_device_ids=true, to_apply=%region_21.22 | all-reduce | flops 1 | bytes 8 | tf_op jit(solution)/shard_map/psum | solution.py:111
  387.3 10.1 %all-reduce = (f32[64]{0:T(128)S(1)}, f32[64]{0:T(128)S(1)}) all-reduce(f32[64]{0:T(128)S(1)} %get-tuple-element.7, f32[64]{0:T(128)S(1)} %get-tuple-element.8), channel_id=1, replica_groups=mesh['row'=8,'col'=4] {'col'}, use_global_device_ids=true, to_apply=%region_15.16 | all-reduce | flops 128 | bytes 1024 | tf_op jit(solution)/shard_map/psum | solution.py:101
  397.5 0.6 broadcast_multiply_fusion.2
  398.1 2.0 fusion.20
  400.1 8.7 %broadcast_multiply_fusion = f32[1536,1536]{1,0:T(8,128)} fusion(f32[1536,1536]{1,0:T(8,128)} %get-tuple-element.31, f32[]{:T(128)S(6)} %min.3), kind=kLoop, calls=%fused_computation.3 | loop fusion | flops 2359296 | bytes 18874372 | tf_op jit(solution)/shard_map/mul | solution.py:116
  408.8 4.8 %broadcast_multiply_fusion.1 = f32[1536,1536]{1,0:T(8,128)} fusion(f32[1536,1536]{1,0:T(8,128)S(1)} %bitcast.13, f32[]{:T(128)S(6)} %min.3), kind=kLoop, calls=%fused_computation.4 | loop fusion | flops 2359296 | bytes 18874372 | tf_op jit(solution)/shard_map/mul | solution.py:116
  413.6 1.7 fusion.27
  (38 shorter events, 0.4 us)
Async XLA Ops:
  7.2 30.5 %all-gather.12.cloned.1.call-start = ((), (), s32[]{:S(2)}) async-start(), calls=%async_computation.9 | async-start | bytes 1769472 | tf_op jit(solution)/shard_map/all_gather | solution.py:82
  7.9 56.4 %all-gather.6.cloned.1.call-start = ((), (), s32[]{:S(2)}) async-start(), calls=%async_computation.4 | async-start | bytes 1769472 | tf_op jit(solution)/shard_map/all_gather | solution.py:45
  23.6 67.3 %all-gather.8.cloned.1.call-start = ((), (), s32[]{:S(2)}) async-start(), calls=%async_computation.5 | async-start | bytes 1769472 | tf_op jit(solution)/shard_map/all_gather | solution.py:46
  24.3 113.1 %reduce-scatter.9.cloned.1.call-start = ((), (), s32[]{:S(2)}) async-start(), calls=%async_computation.10 | async-start | bytes 3932160 | tf_op jit(solution)/shard_map/reduce_scatter | solution.py:83
  44.8 166.1 %reduce-scatter.5.cloned.1.call-start = ((), (), s32[]{:S(2)}) async-start(), calls=%async_computation.6 | async-start | bytes 7864320 | tf_op jit(solution)/shard_map/reduce_scatter | solution.py:49
  99.1 165.8 %all-gather.10.cloned.1.call-start = ((), (), s32[]{:S(2)}) async-start(), calls=%async_computation.7 | async-start | bytes 1966080 | tf_op jit(solution)/shard_map/all_gather | solution.py:75
  213.9 72.8 %all-gather.14.cloned.1.call-start = ((), (), s32[]{:S(2)}) async-start(), calls=%async_computation.12 | async-start | bytes 1966080 | tf_op jit(solution)/shard_map/all_gather | solution.py:87
  213.9 13.0 %collective-permute-start = (bf16[128,1536]{1,0:T(8,128)(2,1)S(1)}, bf16[128,1536]{1,0:T(8,128)(2,1)S(1)}, u32[]{:S(2)}, u32[]{:S(2)}) collective-permute-start(bf16[128,1536]{1,0:T(8,128)(2,1)S(1)} %get-tuple-element.20), channel_id=1, source_target_pairs={{0,1},{1,2},{2,3},{3,0},{4,5},{5,6},{6,7},{7,4},{8,9},{9,10},{10,1... | collective-permute-start | bytes 1179656 | tf_op jit(solution)/shard_map/ppermute | solution.py:90
  227.0 11.3 %collective-permute-start.1 = (bf16[128,1536]{1,0:T(8,128)(2,1)S(1)}, bf16[128,1536]{1,0:T(8,128)(2,1)S(1)}, u32[]{:S(2)}, u32[]{:S(2)}) collective-permute-start(bf16[128,1536]{1,0:T(8,128)(2,1)S(1)} %collective-permute-done), channel_id=1, source_target_pairs={{0,1},{1,2},{2,3},{3,0},{4,5},{5,6},{6,7},{7,4},{8,9},{9,10},{10,1... | collective-permute-start | bytes 1179656 | tf_op jit(solution)/shard_map/ppermute | solution.py:90
  238.2 17.8 %collective-permute-start.2 = (bf16[128,1536]{1,0:T(8,128)(2,1)S(1)}, bf16[128,1536]{1,0:T(8,128)(2,1)S(1)}, u32[]{:S(2)}, u32[]{:S(2)}) collective-permute-start(bf16[128,1536]{1,0:T(8,128)(2,1)S(1)} %collective-permute-done.1), channel_id=1, source_target_pairs={{0,1},{1,2},{2,3},{3,0},{4,5},{5,6},{6,7},{7,4},{8,9},{9,10},{10,1... | collective-permute-start | bytes 1179656 | tf_op jit(solution)/shard_map/ppermute | solution.py:90
  239.1 90.2 %reduce-scatter.11.cloned.1.call-start = ((), (), s32[]{:S(2)}) async-start(), calls=%async_computation.11 | async-start | bytes 3538944 | tf_op jit(solution)/shard_map/reduce_scatter | solution.py:97
  256.3 1.7 copy-start.4
  264.7 148.9 %reduce-scatter.7.cloned.1.call-start = ((), (), s32[]{:S(2)}) async-start(), calls=%async_computation.8 | async-start | bytes 3538944 | tf_op jit(solution)/shard_map/reduce_scatter | solution.py:79
  272.1 1.9 copy-start.5
  281.4 47.9 %copy-start = (bf16[64,1536]{1,0:T(8,128)(2,1)S(1)}, bf16[64,1536]{1,0:T(8,128)(2,1)}, u32[]{:S(2)}) copy-start(bf16[64,1536]{1,0:T(8,128)(2,1)} %param.7) | copy-start | bytes 589828
  281.4 47.9 %copy-start.3 = (f32[1536]{0:T(1024)S(1)}, f32[1536]{0:T(1024)}, u32[]{:S(2)}) copy-start(f32[1536]{0:T(1024)} %param.9) | copy-start | bytes 18436
  281.4 116.6 %copy-start.2 = (bf16[64,1536]{1,0:T(8,128)(2,1)S(1)}, bf16[64,1536]{1,0:T(8,128)(2,1)}, u32[]{:S(2)}) copy-start(bf16[64,1536]{1,0:T(8,128)(2,1)} %param.8) | copy-start | bytes 589828
  398.1 10.7 %slice-start = ((s8[9437184]{0:T(1024)(128)(4,1)}), s8[4194304]{0:T(1024)(128)(4,1)S(1)}, s32[]{:S(2)}) async-start(s8[9437184]{0:T(1024)(128)(4,1)} %bitcast.12), calls=%async_computation.13 | async-start | bytes 8388608
  400.1 8.7 %slice-start.1 = ((s8[9437184]{0:T(1024)(128)(4,1)}), s8[4194304]{0:T(1024)(128)(4,1)S(1)}, s32[]{:S(2)}) async-start(s8[9437184]{0:T(1024)(128)(4,1)} %bitcast.12), calls=%async_computation.14 | async-start | bytes 8388608
  400.1 8.7 %slice-start.2 = ((s8[9437184]{0:T(1024)(128)(4,1)}), s8[1048576]{0:T(1024)(128)(4,1)S(1)}, s32[]{:S(2)}) async-start(s8[9437184]{0:T(1024)(128)(4,1)} %bitcast.12), calls=%async_computation.15 | async-start | bytes 2097152
  408.8 4.8 %copy-start.1 = (bf16[64,1536]{1,0:T(8,128)(2,1)S(1)}, bf16[64,1536]{1,0:T(8,128)(2,1)}, u32[]{:S(2)}) copy-start(bf16[64,1536]{1,0:T(8,128)(2,1)} %param.6) | copy-start | bytes 589828
Sparse Core Ops, SparseCore 0:
  9.6 27.9 all-gather.11
  39.8 24.3 all-gather.5
  66.5 24.3 all-gather.7
  94.3 43.0 reduce-scatter.8
  140.8 70.0 reduce-scatter.4
  214.0 40.0 all-gather.9
  255.9 30.7 all-gather.13
  289.0 40.3 reduce-scatter.10
  331.7 39.8 reduce-scatter.6
